TPU v7x, 256 devices: a whole 4x4x8 slice. The times are simulated.
256 devices in a mesh: gx: 4 (over x), gy: 4 (over y_lo, core), zt: 16 (over y_hi, z).
Axes of the slice: x: 4, y: 4 (y_hi: 2, y_lo: 2; y = y_hi * 2 + y_lo), z: 8, core: 2. Of those that a mesh axis runs over, the one named last changes fastest.
Arguments:
- gauge_links: float32 [4, 2, 3, 3, 8, 32, 2048], P(None, None, None, None, 'gx', 'gy', 'zt'), may hold values from -1 to 1, as said below
- momenta: float32 [4, 2, 3, 3, 8, 32, 2048], P(None, None, None, None, 'gx', 'gy', 'zt'), may hold values from -4 to 4, as said below
Outputs:
- new_links: float32 [4, 2, 3, 3, 8, 32, 2048], P(None, None, None, None, 'gx', 'gy', 'zt')
- new_momenta: float32 [4, 2, 3, 3, 8, 32, 2048], P(None, None, None, None, 'gx', 'gy', 'zt')
- plaquette: float32 [], replicated
Inputs may be any that keep to these rules, and one draw needn't show every extreme that they name: `gauge_links`: every link is a unitary 3 x 3 complex matrix. `momenta`: every momentum is an antihermitian traceless 3 x 3 complex matrix.
All inputs are finite; a program needn't handle non-finite values.
Results may differ from a plain program's by a relative error of at most 0.0001.
Values sent between devices are 32-bit elements; how exact they have to be, the bound alone decides.
A program may use at most 128 MiB of HBM per device.

v0:
```python
import jax
import jax.numpy as jnp
from jax import lax
from jax.experimental import pallas as pl
from jax.experimental.pallas import tpu as pltpu
from jax.sharding import PartitionSpec as P

MESH = pl.DeviceIdType.MESH
F32 = jnp.float32
KICK = 0.25
STEP = 0.2
NAMES = ("gx", "gy", "zt")
LEAD = {(0, 1): 1, (0, 2): 2, (0, 3): 3, (1, 2): 2, (1, 3): 1, (2, 3): 2}
OTHER = (lambda k: k + 1, lambda k: k + (k + 1) // 2, lambda k: k + k // 2, lambda k: k)


def load_matrix(ref, lead, x):
    return [[(ref[lead + (3 * i + j, x)], ref[lead + (9 + 3 * i + j, x)]) for j in range(3)] for i in range(3)]


def add(a, b):
    return b if a is None else a + b


def product(a, b):
    out = []
    for i in range(3):
        line = []
        for j in range(3):
            re, im = None, None
            for k in range(3):
                ar, ai = a[i][k]
                br, bi = b[k][j]
                re = add(re, ar * br - ai * bi)
                im = add(im, ar * bi + ai * br)
            line.append((re, im))
        out.append(line)
    return out


def dagger_entry(x, y, i, j):
    re, im = None, None
    for k in range(3):
        ar, ai = x[i][k]
        br, bi = y[j][k]
        re = add(re, ar * br + ai * bi)
        im = add(im, ai * br - ar * bi)
    return re, im


def twice_traceless(x, y):
    diag = []
    for i in range(3):
        im = None
        for k in range(3):
            ar, ai = x[i][k]
            br, bi = y[i][k]
            im = add(im, ai * br - ar * bi)
        diag.append(im)
    mean = (diag[0] + diag[1] + diag[2]) * (2.0 / 3.0)
    out = [diag[0] + diag[0] - mean, diag[1] + diag[1] - mean]
    for i, j in ((0, 1), (0, 2), (1, 2)):
        pr, pi = dagger_entry(x, y, i, j)
        qr, qi = dagger_entry(x, y, j, i)
        out += [pr - qr, pi + qi]
    return out


def real_trace(x, y):
    total = None
    for i in range(3):
        for k in range(3):
            ar, ai = x[i][k]
            br, bi = y[i][k]
            total = add(total, ar * br + ai * bi)
    return total


def conjugated(d, t):
    d0, d1, ur, ui, vr, vi, wr, wi = t
    d2 = -(d0 + d1)

    def column(j):
        (ar, ai), (br, bi), (cr, ci) = d[0][j], d[1][j], d[2][j]
        first = (
            ur * br - ui * bi + (vr * cr - vi * ci) - d0 * ai,
            ur * bi + ui * br + (vr * ci + vi * cr) + d0 * ar,
        )
        second = (
            wr * cr - wi * ci - (ur * ar + ui * ai) - d1 * bi,
            wr * ci + wi * cr + (ui * ar - ur * ai) + d1 * br,
        )
        third = (
            -(vr * ar + vi * ai) - (wr * br + wi * bi) - d2 * ci,
            (vi * ar - vr * ai) + (wi * br - wr * bi) + d2 * cr,
        )
        return first, second, third

    def imag(i, col):
        total = None
        for k in range(3):
            ar, ai = d[k][i]
            total = add(total, ar * col[k][1] - ai * col[k][0])
        return total

    def entry(i, col):
        re, im = None, None
        for k in range(3):
            ar, ai = d[k][i]
            br, bi = col[k]
            re = add(re, ar * br + ai * bi)
            im = add(im, ar * bi - ai * br)
        return re, im

    zero = column(0)
    e0 = imag(0, zero)
    one = column(1)
    e1 = imag(1, one)
    u = entry(0, one)
    two = column(2)
    v = entry(0, two)
    w = entry(1, two)
    return [e0, e1, u[0], u[1], v[0], v[1], w[0], w[1]]


def cayley(h, scale):
    a0, a1, ur, ui, vr, vi, wr, wi = [scale * part for part in h]
    a2 = -(a0 + a1)
    uu = ur * ur + ui * ui
    vv = vr * vr + vi * vi
    ww = wr * wr + wi * wi
    s00, s11, s22 = a0 * a0, a1 * a1, a2 * a2
    one_s = 1.0 + (0.5 * (s00 + s11 + s22) + (uu + vv + ww))
    uwr, uwi = ur * wr - ui * wi, ur * wi + ui * wr
    det_h = a0 * a1 * a2 + 2.0 * (uwi * vr - uwr * vi) - a0 * ww - a1 * vv - a2 * uu
    scale2 = 2.0 / (one_s * one_s + det_h * det_h)
    qr, qi = one_s * scale2, -(det_h * scale2)
    pr, pi = a2 * ui - (vr * wr + vi * wi), -(a2 * ur) - (vi * wr - vr * wi)
    rr, ri = a1 * vi + uwr, uwi - a1 * vr
    tr, ti = a0 * wi - (ur * vr + ui * vi), -(a0 * wr) - (ur * vi - ui * vr)
    rows = [
        [(one_s - (s00 + uu + vv), a0), (ur + pr, ui + pi), (vr + rr, vi + ri)],
        [(pr - ur, ui - pi), (one_s - (s11 + uu + ww), a1), (wr + tr, wi + ti)],
        [(rr - vr, vi - ri), (tr - wr, wi - ti), (one_s - (s22 + vv + ww), a2)],
    ]
    out = []
    for i in range(3):
        line = []
        for j in range(3):
            br, bi = rows[i][j]
            re, im = br * qr - bi * qi, br * qi + bi * qr
            line.append((re - 1.0 if i == j else re, im))
        out.append(line)
    return out


PARTS = (9, 13, 1, 10, 2, 11, 5, 14)


def kernel(
    sizes, gauge, momenta, new_links, new_momenta, plaquette,
    links, shifted, row_out, row_in, lane_out, lane_in,
    loops, lower, low_row_out, low_row_in, low_lane_out, low_lane_in,
    moment, final, traces, gather,
    load_sem, x_send, x_recv, y_send, y_recv, z_send, z_recv,
    lx_send, lx_recv, ly_send, ly_recv, lz_send, lz_recv, sum_send, sum_recv, store_sem,
):
    me = [lax.axis_index(name) for name in NAMES]

    def peer(axis, offset):
        return {NAMES[axis]: lax.rem(me[axis] + (offset + sizes[axis]), sizes[axis])}

    barrier = pltpu.get_barrier_semaphore()
    count = 0
    for axis in range(3):
        for offset in range(1, sizes[axis]):
            pl.semaphore_signal(barrier, inc=1, device_id=peer(axis, offset), device_id_type=MESH)
            count += 1

    loads = []
    for m in range(4):
        loads.append(pltpu.make_async_copy(gauge.at[m], links.at[0, m], load_sem.at[m]))
    for n in (1, 2, 3):
        loads.append(pltpu.make_async_copy(gauge.at[n, :, 1], shifted.at[0, 0, n, :, 0], load_sem.at[3 + n]))
    loads.append(pltpu.make_async_copy(momenta, moment, load_sem.at[7]))
    for copy in loads:
        copy.start()

    lane = lax.broadcasted_iota(jnp.int32, (8, 128), 1)
    row = lax.broadcasted_iota(jnp.int32, (8, 128), 0)
    low = lane < 64
    time = lax.rem(lane, 64)
    last_time = time == 63
    first_time = time == 0
    last_row = row == 7
    first_row = row == 0

    for copy in loads[:4]:
        copy.wait()

    def x_copy(ph, n):
        return pltpu.make_async_remote_copy(
            src_ref=links.at[ph, n, :, 0], dst_ref=shifted.at[ph, 0, n, :, 1],
            send_sem=x_send.at[ph, n], recv_sem=x_recv.at[ph, n],
            device_id=peer(0, -1), device_id_type=MESH)

    def y_copy(ph):
        return pltpu.make_async_remote_copy(
            src_ref=row_out.at[ph], dst_ref=row_in.at[ph],
            send_sem=y_send.at[ph], recv_sem=y_recv.at[ph],
            device_id=peer(1, -1), device_id_type=MESH)

    def z_copy(ph, k):
        return pltpu.make_async_remote_copy(
            src_ref=lane_out.at[ph, k], dst_ref=lane_in.at[ph, k],
            send_sem=z_send.at[ph, k], recv_sem=z_recv.at[ph, k],
            device_id=peer(2, -1), device_id_type=MESH)

    def lx_copy(ph, m):
        return pltpu.make_async_remote_copy(
            src_ref=lower.at[ph, 0, m, :, 2], dst_ref=lower.at[ph, 0, m, :, 0],
            send_sem=lx_send.at[ph, m], recv_sem=lx_recv.at[ph, m],
            device_id=peer(0, 1), device_id_type=MESH)

    def ly_copy(ph):
        return pltpu.make_async_remote_copy(
            src_ref=low_row_out.at[ph], dst_ref=low_row_in.at[ph],
            send_sem=ly_send.at[ph], recv_sem=ly_recv.at[ph],
            device_id=peer(1, 1), device_id_type=MESH)

    def lz_copy(ph, k):
        return pltpu.make_async_remote_copy(
            src_ref=low_lane_out.at[ph, k], dst_ref=low_lane_in.at[ph, k],
            send_sem=lz_send.at[ph, k], recv_sem=lz_recv.at[ph, k],
            device_id=peer(2, 1), device_id_type=MESH)

    def plane(ph, m, n, x, slot):
        a = load_matrix(links, (ph, m), x)
        b = load_matrix(shifted, (ph, m, n), x)
        left = product(a, b)
        d = load_matrix(links, (ph, n), x)
        c = load_matrix(shifted, (ph, n, m), x)
        right = product(d, c)
        t = twice_traceless(left, right)
        if ph == 1:
            traces[slot] = real_trace(left, right)
        for p in range(8):
            loops[m, n, p, x] = t[p]
        for p, value in enumerate(conjugated(d, t)):
            lower[ph, n, m, p, x + 1] = value
        for p, value in enumerate(conjugated(a, t)):
            lower[ph, m, n, p, x + 1] = value

    def pairs(body):
        def step(i, _):
            body(i // 2, lax.rem(i, 2))
            return 0
        lax.fori_loop(0, 6, step, 0)

    def sum_copy(axis, offset):
        return pltpu.make_async_remote_copy(
            src_ref=gather.at[axis, me[axis]], dst_ref=gather.at[axis, me[axis]],
            send_sem=sum_send.at[axis, offset], recv_sem=sum_recv.at[axis, offset],
            device_id=peer(axis, offset), device_id_type=MESH)

    for ph in range(2):
        def pack_rows(k, x):
            n = OTHER[1](k)
            for c in range(18):
                row_out[ph, k, c, x] = links[ph, n, c, x, 0:1, :]
        pairs(pack_rows)

        def pack_lanes(k, _):
            n = OTHER[2](k)
            for c in range(18):
                v0 = links[ph, n, c, 0]
                v1 = links[ph, n, c, 1]
                r0 = pltpu.roll(v0, 64, 1)
                lane_out[ph, k, c] = jnp.where(low, v1, r0)
                shifted[ph, 2, n, c, 0] = r0
                shifted[ph, 2, n, c, 1] = pltpu.roll(v1, 64, 1)
            return 0
        lax.fori_loop(0, 3, pack_lanes, 0)

        if ph == 0:
            pl.semaphore_wait(barrier, count)
        for n in (1, 3, 2):
            x_copy(ph, n).start()
        y_copy(ph).start()
        for k in range(3):
            z_copy(ph, k).start()

        def shift_time(k, x):
            for c in range(18):
                v = links[ph, k, c, x]
                shifted[ph, 3, k, c, x] = jnp.where(last_time, pltpu.roll(v, 63, 1), pltpu.roll(v, 127, 1))
        pairs(shift_time)
        if ph == 0:
            for copy in loads[4:7]:
                copy.wait()
        plane(ph, 3, 0, 0, 0)

        y_copy(ph).wait_recv()

        def shift_rows(k, x):
            n = OTHER[1](k)
            for c in range(18):
                v = links[ph, n, c, x]
                edge = jnp.broadcast_to(row_in[ph, k, c, x], (8, 128))
                shifted[ph, 1, n, c, x] = jnp.where(last_row, edge, pltpu.roll(v, 7, 0))
        pairs(shift_rows)

        def y_planes(i, _):
            plane(ph, 1, 3 - 3 * (i // 2), lax.rem(i, 2), 1 + i)
            return 0
        lax.fori_loop(0, 3, y_planes, 0)

        x_copy(ph, 1).wait_recv()
        x_copy(ph, 3).wait_recv()

        def x_planes(i, _):
            plane(ph, 1 + 2 * i, 0, 1, 4 + i)
            return 0
        lax.fori_loop(0, 2, x_planes, 0)
        x_copy(ph, 2).wait_recv()
        for k in range(3):
            z_copy(ph, k).wait_recv()

        def shift_lanes(k, _):
            n = OTHER[2](k)
            for c in range(18):
                edge = lane_in[ph, k, c]
                shifted[ph, 2, n, c, 0] = jnp.where(low, shifted[ph, 2, n, c, 0], edge)
                shifted[ph, 2, n, c, 1] = jnp.where(low, shifted[ph, 2, n, c, 1], pltpu.roll(edge, 64, 1))
            return 0
        lax.fori_loop(0, 3, shift_lanes, 0)

        pairs(lambda k, x: plane(ph, 2, OTHER[2](k), x, 6 + 2 * k + x))

        if ph == 1:
            total = traces[0]
            for slot in range(1, 12):
                total = total + traces[slot]
            gather[0, me[0]] = jnp.sum(total, axis=0, keepdims=True)
            for offset in range(1, sizes[0]):
                sum_copy(0, offset).start()

        for m in (1, 2, 3):
            lx_copy(ph, m).start()

        def pack_low_rows(k, x):
            m = OTHER[1](k)
            for p in range(8):
                low_row_out[ph, k, p, x] = lower[ph, 1, m, p, x + 1, 7:8, :]
        pairs(pack_low_rows)

        def pack_low_lanes(k, _):
            m = OTHER[2](k)
            for p in range(8):
                low_lane_out[ph, k, p] = jnp.where(low, pltpu.roll(lower[ph, 2, m, p, 1], 64, 1), lower[ph, 2, m, p, 2])
            return 0
        lax.fori_loop(0, 3, pack_low_lanes, 0)
        ly_copy(ph).start()
        for k in range(3):
            lz_copy(ph, k).start()

        if ph == 0:
            loads[7].wait()
        ly_copy(ph).wait_recv()
        for m in (1, 2, 3):
            lx_copy(ph, m).wait_recv()
        for k in range(3):
            lz_copy(ph, k).wait_recv()

        def force(x, _):
            for m in range(4):
                total = [None] * 8
                for n in range(4):
                    if n == m:
                        continue
                    lead = LEAD[min(m, n), max(m, n)]
                    first, second = (m, n) if lead == m else (n, m)
                    for p in range(8):
                        here = loops[first, second, p, x]
                        if n == 0:
                            below = lower[ph, 0, m, p, x]
                        else:
                            value = lower[ph, n, m, p, x + 1]
                            if n == 1:
                                k = {0: 0, 2: 1, 3: 2}[m]
                                edge = jnp.broadcast_to(low_row_in[ph, k, p, x], (8, 128))
                                below = jnp.where(first_row, edge, pltpu.roll(value, 1, 0))
                            elif n == 2:
                                k = {0: 0, 1: 1, 3: 2}[m]
                                edge = pltpu.roll(low_lane_in[ph, k, p], 64 * x, 1)
                                below = jnp.where(low, edge, pltpu.roll(value, 64, 1))
                            else:
                                below = jnp.where(first_time, pltpu.roll(value, 65, 1), pltpu.roll(value, 1, 1))
                        term = here - below if lead == m else below - here
                        total[p] = add(total[p], term)
                if ph == 0:
                    for p in range(8):
                        moment[m, PARTS[p], x] = moment[m, PARTS[p], x] - (0.5 * KICK) * total[p]
                else:
                    h = [moment[m, PARTS[p], x] - (0.5 * KICK) * total[p] for p in range(8)]
                    for p in range(8):
                        final[m, PARTS[p], x] = h[p]
                    final[m, 17, x] = -(h[0] + h[1])
                    for c, p in ((3, 2), (6, 4), (7, 6)):
                        final[m, c, x] = -h[p]
                        final[m, 9 + c, x] = h[p + 1]
                    for c in (0, 4, 8):
                        final[m, c, x] = jnp.zeros((8, 128), F32)
            return 0
        lax.fori_loop(0, 2, force, 0)

        if ph == 0:
            def update(i, _):
                m, x = i // 2, lax.rem(i, 2)
                u = cayley([moment[m, p, x] for p in PARTS], 0.5 * STEP)
                new = product(u, load_matrix(links, (0, m), x))
                for i3 in range(3):
                    for j3 in range(3):
                        for part in range(2):
                            links[1, m, 9 * part + 3 * i3 + j3, x] = new[i3][j3][part]
                return 0
            lax.fori_loop(0, 8, update, 0)

            def copy_x(k, _):
                for c in range(18):
                    shifted[1, 0, k + 1, c, 0] = links[1, k + 1, c, 1]
                return 0
            lax.fori_loop(0, 3, copy_x, 0)
            store_links = pltpu.make_async_copy(links.at[1], new_links, store_sem.at[0])
            store_links.start()

    store_momenta = pltpu.make_async_copy(final, new_momenta, store_sem.at[1])
    store_momenta.start()
    for axis in range(3):
        for offset in range(1, sizes[axis]):
            sum_copy(axis, offset).wait_recv()
        total = gather[axis, 0]
        for source in range(1, sizes[axis]):
            total = total + gather[axis, source]
        if axis < 2:
            gather[axis + 1, me[axis + 1]] = total
            for offset in range(1, sizes[axis + 1]):
                sum_copy(axis + 1, offset).start()
    volume = 72.0 * (2 * 8 * 128) * (sizes[0] * sizes[1] * sizes[2])
    plaquette[0, 0] = jnp.sum(total) * (4.0 / volume)

    for ph in range(2):
        for n in (1, 2, 3):
            x_copy(ph, n).wait_send()
            lx_copy(ph, n).wait_send()
        y_copy(ph).wait_send()
        ly_copy(ph).wait_send()
        for k in range(3):
            z_copy(ph, k).wait_send()
            lz_copy(ph, k).wait_send()
    for axis in range(3):
        for offset in range(1, sizes[axis]):
            sum_copy(axis, offset).wait_send()
    store_links.wait()
    store_momenta.wait()


def solution(mesh):
    sizes = tuple(mesh.shape[name] for name in NAMES)
    spec = P(None, None, None, None, "gx", "gy", "zt")

    def step(gauge, momenta):
        shape = gauge.shape
        flat = (4, 18) + shape[4:]
        field = jax.ShapeDtypeStruct(flat, F32)
        dma = pltpu.SemaphoreType.DMA
        any_space = pl.BlockSpec(memory_space=pl.ANY)
        links, final, plaquette = pl.pallas_call(
            lambda *refs: kernel(sizes, *refs),
            name="md_step",
            out_shape=(field, field, jax.ShapeDtypeStruct((1, 1), F32)),
            in_specs=[any_space] * 2,
            out_specs=(any_space, any_space, pl.BlockSpec(memory_space=pltpu.SMEM)),
            scratch_shapes=[
                pltpu.VMEM((2, 4, 18, 2, 8, 128), F32),
                pltpu.VMEM((2, 4, 4, 18, 2, 8, 128), F32),
                pltpu.VMEM((2, 3, 18, 2, 1, 128), F32),
                pltpu.VMEM((2, 3, 18, 2, 1, 128), F32),
                pltpu.VMEM((2, 3, 18, 8, 128), F32),
                pltpu.VMEM((2, 3, 18, 8, 128), F32),
                pltpu.VMEM((4, 4, 8, 2, 8, 128), F32),
                pltpu.VMEM((2, 4, 4, 8, 3, 8, 128), F32),
                pltpu.VMEM((2, 3, 8, 2, 1, 128), F32),
                pltpu.VMEM((2, 3, 8, 2, 1, 128), F32),
                pltpu.VMEM((2, 3, 8, 8, 128), F32),
                pltpu.VMEM((2, 3, 8, 8, 128), F32),
                pltpu.VMEM((4, 18, 2, 8, 128), F32),
                pltpu.VMEM((4, 18, 2, 8, 128), F32),
                pltpu.VMEM((12, 8, 128), F32),
                pltpu.VMEM((3, max(sizes), 1, 128), F32),
                dma((8,)),
                dma((2, 4)), dma((2, 4)), dma((2,)), dma((2,)), dma((2, 3)), dma((2, 3)),
                dma((2, 4)), dma((2, 4)), dma((2,)), dma((2,)), dma((2, 3)), dma((2, 3)),
                dma((3, max(sizes))), dma((3, max(sizes))), dma((2,)),
            ],
            compiler_params=pltpu.CompilerParams(collective_id=0, has_side_effects=True, vmem_limit_bytes=48 * 1024 * 1024),
        )(gauge.reshape(flat), momenta.reshape(flat))
        return links.reshape(shape), final.reshape(shape), plaquette[0, 0]

    return jax.shard_map(step, mesh=mesh, in_specs=(spec, spec), out_specs=(spec, spec, P()), check_vma=False)
```

profile of v0, /device:TPU:1, one launch (start us, length us, event | category | flops | bytes accessed | tf_op | source)
XLA Modules:
  0.0 55.7 jit_solution(3245082114776854498)
XLA Ops:
  0.6 0.0 copy-start
  0.6 1.1 %copy-done = f32[4,2,3,3,2,8,128]{6,5,4,3,2,1,0:T(8,128)S(1)} copy-done((f32[4,2,3,3,2,8,128]{6,5,4,3,2,1,0:T(8,128)S(1)}, f32[4,2,3,3,2,8,128]{6,5,4,3,2,1,0:T(8,128)}, u32[]{:S(2)}) %copy-start) | copy-done | bytes 589848
  1.7 0.0 copy-start.1
  1.7 1.1 %copy-done.1 = f32[4,2,3,3,2,8,128]{6,5,4,3,2,1,0:T(8,128)S(1)} copy-done((f32[4,2,3,3,2,8,128]{6,5,4,3,2,1,0:T(8,128)S(1)}, f32[4,2,3,3,2,8,128]{6,5,4,3,2,1,0:T(8,128)}, u32[]{:S(2)}) %copy-start.1) | copy-done | bytes 589848
  2.8 49.6 %md_step.1 = (f32[4,18,2,8,128]{4,3,2,1,0:T(8,128)S(1)}, f32[4,18,2,8,128]{4,3,2,1,0:T(8,128)S(1)}, f32[1,1]{1,0:T(1,128)}) custom-call(f32[4,18,2,8,128]{4,3,2,1,0:T(8,128)S(1)} %bitcast.5, f32[4,18,2,8,128]{4,3,2,1,0:T(8,128)S(1)} %bitcast.6), custom_call_target="tpu_custom_call" | custom-call | tf_op jit(solution)/shard_map/md_step/pallas_call | solution.py:478
  52.3 0.8 %copy.8 = f32[4,2,3,3,2,8,128]{6,5,4,3,2,1,0:T(8,128)} copy(f32[4,2,3,3,2,8,128]{6,5,4,3,2,1,0:T(8,128)S(1)} %bitcast.8) | data formatting | bytes 1179648
  53.1 0.8 %copy.9 = f32[4,2,3,3,2,8,128]{6,5,4,3,2,1,0:T(8,128)} copy(f32[4,2,3,3,2,8,128]{6,5,4,3,2,1,0:T(8,128)S(1)} %bitcast.7) | data formatting | bytes 1179648
Async XLA Ops:
  0.6 1.1 %copy-start = (f32[4,2,3,3,2,8,128]{6,5,4,3,2,1,0:T(8,128)S(1)}, f32[4,2,3,3,2,8,128]{6,5,4,3,2,1,0:T(8,128)}, u32[]{:S(2)}) copy-start(f32[4,2,3,3,2,8,128]{6,5,4,3,2,1,0:T(8,128)} %param.2) | copy-start | bytes 1769476
  1.7 1.1 %copy-start.1 = (f32[4,2,3,3,2,8,128]{6,5,4,3,2,1,0:T(8,128)S(1)}, f32[4,2,3,3,2,8,128]{6,5,4,3,2,1,0:T(8,128)}, u32[]{:S(2)}) copy-start(f32[4,2,3,3,2,8,128]{6,5,4,3,2,1,0:T(8,128)} %param.3) | copy-start | bytes 1769476
where the time goes:
time: 55.9 us; the launch traced here: 55.7 us
  Pallas kernels  49.6 us (89%)
  local copies, waits for them, and re-layouts  3.75 us (7%)
  between operations  2.41 us (4%)
    pallas_call x1, Pallas kernels, step(): pl.pallas_call(lambda *refs: kernel(sizes, *refs), name='md_step', out_sh...  49.6 us
    unnamed x6, local copies, waits for them, and re-layouts  3.75 us

commit v1 on v0

v1 whole, which is shorter than its diff:
```python
import jax
import jax.numpy as jnp
from jax import lax
from jax.experimental import pallas as pl
from jax.experimental.pallas import tpu as pltpu
from jax.sharding import PartitionSpec as P

MESH = pl.DeviceIdType.MESH
F32 = jnp.float32
KICK = 0.25
STEP = 0.2
NAMES = ("gx", "gy", "zt")
LEAD = {(0, 1): 1, (0, 2): 2, (0, 3): 3, (1, 2): 2, (1, 3): 1, (2, 3): 3}


def load_matrix(ref, lead, *rest):
    return [[(ref[(*lead, 3 * i + j, *rest)], ref[(*lead, 9 + 3 * i + j, *rest)]) for j in range(3)] for i in range(3)]


def store_matrix(ref, lead, rest, value):
    for i in range(3):
        for j in range(3):
            for part in range(2):
                ref[(*lead, 9 * part + 3 * i + j, *rest)] = value[i][j][part]


def add(a, b):
    return b if a is None else a + b


def product(a, b):
    out = []
    for i in range(3):
        line = []
        for j in range(3):
            re, im = None, None
            for k in range(3):
                ar, ai = a[i][k]
                br, bi = b[k][j]
                re = add(re, ar * br - ai * bi)
                im = add(im, ar * bi + ai * br)
            line.append((re, im))
        out.append(line)
    return out


def dagger(a):
    return [[(a[j][i][0], -a[j][i][1]) for j in range(3)] for i in range(3)]


def dagger_product(a, b):
    out = []
    for i in range(3):
        line = []
        for j in range(3):
            re, im = None, None
            for k in range(3):
                ar, ai = a[k][i]
                br, bi = b[k][j]
                re = add(re, ar * br + ai * bi)
                im = add(im, ar * bi - ai * br)
            line.append((re, im))
        out.append(line)
    return out


def dagger_entry(x, y, i, j):
    re, im = None, None
    for k in range(3):
        ar, ai = x[i][k]
        br, bi = y[j][k]
        re = add(re, ar * br + ai * bi)
        im = add(im, ai * br - ar * bi)
    return re, im


def twice_traceless(x, y):
    diag = []
    for i in range(3):
        im = None
        for k in range(3):
            ar, ai = x[i][k]
            br, bi = y[i][k]
            im = add(im, ai * br - ar * bi)
        diag.append(im)
    mean = (diag[0] + diag[1] + diag[2]) * (2.0 / 3.0)
    out = [diag[0] + diag[0] - mean, diag[1] + diag[1] - mean]
    for i, j in ((0, 1), (0, 2), (1, 2)):
        pr, pi = dagger_entry(x, y, i, j)
        qr, qi = dagger_entry(x, y, j, i)
        out += [pr - qr, pi + qi]
    return out


def real_trace(x, y):
    total = None
    for i in range(3):
        for k in range(3):
            ar, ai = x[i][k]
            br, bi = y[i][k]
            total = add(total, ar * br + ai * bi)
    return total


def conjugated(d, t):
    d0, d1, ur, ui, vr, vi, wr, wi = t
    d2 = -(d0 + d1)

    def column(j):
        (ar, ai), (br, bi), (cr, ci) = d[0][j], d[1][j], d[2][j]
        first = (
            ur * br - ui * bi + (vr * cr - vi * ci) - d0 * ai,
            ur * bi + ui * br + (vr * ci + vi * cr) + d0 * ar,
        )
        second = (
            wr * cr - wi * ci - (ur * ar + ui * ai) - d1 * bi,
            wr * ci + wi * cr + (ui * ar - ur * ai) + d1 * br,
        )
        third = (
            -(vr * ar + vi * ai) - (wr * br + wi * bi) - d2 * ci,
            (vi * ar - vr * ai) + (wi * br - wr * bi) + d2 * cr,
        )
        return first, second, third

    def imag(i, col):
        total = None
        for k in range(3):
            ar, ai = d[k][i]
            total = add(total, ar * col[k][1] - ai * col[k][0])
        return total

    def entry(i, col):
        re, im = None, None
        for k in range(3):
            ar, ai = d[k][i]
            br, bi = col[k]
            re = add(re, ar * br + ai * bi)
            im = add(im, ar * bi - ai * br)
        return re, im

    zero = column(0)
    e0 = imag(0, zero)
    one = column(1)
    e1 = imag(1, one)
    u = entry(0, one)
    two = column(2)
    v = entry(0, two)
    w = entry(1, two)
    return [e0, e1, u[0], u[1], v[0], v[1], w[0], w[1]]


def cayley(h, scale):
    a0, a1, ur, ui, vr, vi, wr, wi = [scale * part for part in h]
    a2 = -(a0 + a1)
    uu = ur * ur + ui * ui
    vv = vr * vr + vi * vi
    ww = wr * wr + wi * wi
    s00, s11, s22 = a0 * a0, a1 * a1, a2 * a2
    one_s = 1.0 + (0.5 * (s00 + s11 + s22) + (uu + vv + ww))
    uwr, uwi = ur * wr - ui * wi, ur * wi + ui * wr
    det_h = a0 * a1 * a2 + 2.0 * (uwi * vr - uwr * vi) - a0 * ww - a1 * vv - a2 * uu
    scale2 = 2.0 / (one_s * one_s + det_h * det_h)
    qr, qi = one_s * scale2, -(det_h * scale2)
    pr, pi = a2 * ui - (vr * wr + vi * wi), -(a2 * ur) - (vi * wr - vr * wi)
    rr, ri = a1 * vi + uwr, uwi - a1 * vr
    tr, ti = a0 * wi - (ur * vr + ui * vi), -(a0 * wr) - (ur * vi - ui * vr)
    rows = [
        [(one_s - (s00 + uu + vv), a0), (ur + pr, ui + pi), (vr + rr, vi + ri)],
        [(pr - ur, ui - pi), (one_s - (s11 + uu + ww), a1), (wr + tr, wi + ti)],
        [(rr - vr, vi - ri), (tr - wr, wi - ti), (one_s - (s22 + vv + ww), a2)],
    ]
    out = []
    for i in range(3):
        line = []
        for j in range(3):
            br, bi = rows[i][j]
            re, im = br * qr - bi * qi, br * qi + bi * qr
            line.append((re - 1.0 if i == j else re, im))
        out.append(line)
    return out


PARTS = (9, 13, 1, 10, 2, 11, 5, 14)
ROWS = (0, 2, 3)


def kernel(
    sizes, gauge, momenta, new_links, final, plaquette,
    old_links, moment, time_ahead, row_ahead, lane_ahead, mixed,
    loops, lower, lower_time,
    row_out, row_in, x_in, lane_out, lane_in, mix_out, mix_in,
    low_row_out, low_row_in, low_lane_out, low_lane_in, time_out, time_in,
    traces, gather_z, gather_rest,
    load_sem, send_sem, recv_sem, z_send, z_recv, rest_send, rest_recv, known_sem,
):
    me = [lax.axis_index(name) for name in NAMES]
    links = (old_links, new_links)
    half = sizes[2] // 2
    my_half, my_z = me[2] // half, lax.rem(me[2], half)

    def peer(axis, offset):
        return {NAMES[axis]: lax.rem(me[axis] + (offset + sizes[axis]), sizes[axis])}

    def z_peer(offset):
        return {"zt": my_half * half + lax.rem(my_z + offset, half)}

    rest = [(i, j, k) for i in range(sizes[0]) for j in range(sizes[1]) for k in range(2) if i + j + k]

    def rest_peer(offset):
        i, j, k = offset
        return {**peer(0, i), **peer(1, j), "zt": lax.rem(my_half + k, 2) * half + my_z}

    barrier = pltpu.get_barrier_semaphore()
    neighbours = [peer(axis, offset) for axis in range(3) for offset in (-1, 1)]
    for device in neighbours:
        pl.semaphore_signal(barrier, inc=1, device_id=device, device_id_type=MESH)

    loads = {m: pltpu.make_async_copy(gauge.at[m], old_links.at[m], load_sem.at[m]) for m in (1, 0, 2, 3)}
    loads[4] = pltpu.make_async_copy(momenta, moment, load_sem.at[4])
    for copy in loads.values():
        copy.start()

    def known(step, *offsets):
        for offset in offsets:
            pl.semaphore_signal(known_sem.at[step], inc=1, device_id=peer(2, offset), device_id_type=MESH)

    lane = lax.broadcasted_iota(jnp.int32, (8, 128), 1)
    row = lax.broadcasted_iota(jnp.int32, (8, 128), 0)
    low = lane < 64
    time = lax.rem(lane, 64)
    last_time = time == 63
    first_time = time == 0
    last_row = row == 7
    first_row = row == 0

    def flip(value):
        return pltpu.roll(value, 64, 1)

    def remote(ph, name):
        now = links[ph]
        number, src, dst, axis, offset = {
            "x1": (0, now.at[1, :, 0], x_in.at[ph, 0], 0, -1),
            "x2": (1, now.at[2, :, 0], x_in.at[ph, 1], 0, -1),
            "y": (2, row_out.at[ph], row_in.at[ph], 1, -1),
            "z0": (3, lane_out.at[ph, 0], lane_in.at[ph, 0], 2, -1),
            "z1": (4, lane_out.at[ph, 1], lane_in.at[ph, 1], 2, -1),
            "mx": (5, mixed.at[ph, 0, :, 2], mixed.at[ph, 0, :, 0], 0, 1),
            "mz": (6, mix_out.at[ph], mix_in.at[ph], 2, 1),
            "lx1": (7, lower.at[ph, 0, 1, :, 2], lower.at[ph, 0, 1, :, 0], 0, 1),
            "lx2": (8, lower.at[ph, 0, 2, :, 2], lower.at[ph, 0, 2, :, 0], 0, 1),
            "ly": (9, low_row_out.at[ph], low_row_in.at[ph], 1, 1),
            "lz0": (10, low_lane_out.at[ph, 0], low_lane_in.at[ph, 0], 2, 1),
            "lz1": (11, low_lane_out.at[ph, 1], low_lane_in.at[ph, 1], 2, 1),
            "tx": (12, lower.at[ph, 0, 3, :, 0], lower.at[ph, 0, 3, :, 2], 0, -1),
            "tz": (13, time_out.at[ph], time_in.at[ph], 2, -1),
        }[name]
        return pltpu.make_async_remote_copy(
            src_ref=src, dst_ref=dst, send_sem=send_sem.at[ph, number], recv_sem=recv_sem.at[ph, number],
            device_id=peer(axis, offset), device_id_type=MESH)

    names = ("x1", "x2", "y", "z0", "z1", "mx", "mz", "lx1", "lx2", "ly", "lz0", "lz1", "tx", "tz")

    def z_sum(offset):
        return pltpu.make_async_remote_copy(
            src_ref=gather_z.at[my_z], dst_ref=gather_z.at[my_z],
            send_sem=z_send.at[offset], recv_sem=z_recv.at[offset],
            device_id=z_peer(offset), device_id_type=MESH)

    my_rest = (me[0] * sizes[1] + me[1]) * 2 + my_half

    def rest_sum(offset):
        number = (offset[0] * sizes[1] + offset[1]) * 2 + offset[2]
        return pltpu.make_async_remote_copy(
            src_ref=gather_rest.at[my_rest], dst_ref=gather_rest.at[my_rest],
            send_sem=rest_send.at[number], recv_sem=rest_recv.at[number],
            device_id=rest_peer(offset), device_id_type=MESH)

    def loop(count, body):
        def step(i, _):
            body(i)
            return 0
        lax.fori_loop(0, count, step, 0)

    def plane(ph, m, n, x, b, c, slot, split=False):
        a = load_matrix(links[ph], (m,), x)
        left = product(a, b)
        d = load_matrix(links[ph], (n,), x)
        right = product(d, c)
        t = twice_traceless(left, right)
        if ph == 1:
            traces[slot] = real_trace(left, right)
        for p in range(8):
            loops[m, n, p, x] = t[p]
        if not split:
            below(ph, m, n, x, a, d, t)

    def below(ph, m, n, x, a, d, t):
        for p, value in enumerate(conjugated(d, t)):
            lower[ph, n, m, p, x + 1] = value
        for p, value in enumerate(conjugated(a, t)):
            lower[ph, m, n, p, x + 1] = value

    def ahead_x(ph, n, x):
        return load_matrix(links[ph], (n,), 1) if x == 0 else load_matrix(x_in, (ph, n - 1))

    def pack_lanes(ph, m):
        for c in range(18):
            v0 = links[ph][m, c, 0]
            v1 = links[ph][m, c, 1]
            r0 = flip(v0)
            lane_out[ph, m, c] = jnp.where(low, v1, r0)
            lane_ahead[m, c, 0] = r0
            lane_ahead[m, c, 1] = flip(v1)

    def send_edges(ph, m):
        if m in (0, 1):
            remote(ph, "z" + str(m)).start()
        if m in (1, 2):
            remote(ph, "x" + str(m)).start()

    def first_half(ph):
        def shift_time(n, x):
            for c in range(18):
                v = links[ph][n, c, x]
                time_ahead[n, c, x] = jnp.where(last_time, pltpu.roll(v, 63, 1), pltpu.roll(v, 127, 1))

        def mix(d, x):
            left = product(load_matrix(links[ph], (3,), x), load_matrix(time_ahead, (d,), x))
            store_matrix(mixed, (ph, d // 2), (x + 1,), dagger_product(load_matrix(links[ph], (d,), x), left))

        loop(2, lambda x: shift_time(2, x))
        loop(2, lambda x: mix(2, x))
        for c in range(18):
            mix_out[ph, c] = jnp.where(low, flip(mixed[ph, 1, c, 1]), mixed[ph, 1, c, 2])
        remote(ph, "mz").start()

        def pack_rows(x):
            for k, n in enumerate(ROWS):
                for c in range(18):
                    row_out[ph, k, c, x] = links[ph][n, c, x, 0:1, :]
        loop(2, pack_rows)
        remote(ph, "y").start()

        loop(4, lambda i: shift_time(i // 2, lax.rem(i, 2)))
        loop(2, lambda x: mix(0, x))
        remote(ph, "mx").start()

        remote(ph, "y").wait_recv()

        def shift_rows(i):
            k, x = i // 2, lax.rem(i, 2)
            n = k + (k + 1) // 2
            for c in range(18):
                v = links[ph][n, c, x]
                edge = jnp.broadcast_to(row_in[ph, k, c, x], (8, 128))
                row_ahead[n, c, x] = jnp.where(last_row, edge, pltpu.roll(v, 7, 0))
        loop(6, shift_rows)

        plane(ph, 1, 0, 0, load_matrix(row_ahead, (0,), 0), ahead_x(ph, 1, 0), 0)
        loop(2, lambda x: plane(
            ph, 1, 3, x, load_matrix(row_ahead, (3,), x), load_matrix(time_ahead, (1,), x), 2 + x))

        remote(ph, "x1").wait_recv()
        plane(ph, 1, 0, 1, load_matrix(row_ahead, (0,), 1), ahead_x(ph, 1, 1), 1)
        remote(ph, "lx1").start()

        def ahead_z(m):
            for c in range(18):
                edge = lane_in[ph, m, c]
                lane_ahead[m, c, 0] = jnp.where(low, lane_ahead[m, c, 0], edge)
                lane_ahead[m, c, 1] = jnp.where(low, lane_ahead[m, c, 1], flip(edge))

        def pack_lower(m):
            for p in range(8):
                low_lane_out[ph, m, p] = jnp.where(low, flip(lower[ph, 2, m, p, 1]), lower[ph, 2, m, p, 2])

        remote(ph, "z1").wait_recv()
        ahead_z(1)
        loop(2, lambda x: plane(
            ph, 2, 1, x, load_matrix(lane_ahead, (1,), x), load_matrix(row_ahead, (2,), x), 4 + x))
        pack_lower(1)
        remote(ph, "lz1").start()
        for k, m in enumerate(ROWS):
            for p in range(8):
                for x in range(2):
                    low_row_out[ph, k, p, x] = lower[ph, 1, m, p, x + 1, 7:8, :]
        remote(ph, "ly").start()

        remote(ph, "mx").wait_recv()
        def seen_x(x):
            m, c = load_matrix(mixed, (ph, 0), x), load_matrix(links[ph], (3,), x)
            if ph == 1:
                traces[6 + x] = real_trace(m, c)
            for p, value in enumerate(twice_traceless(m, c)):
                lower[ph, 0, 3, p, x] = value
        loop(2, seen_x)
        remote(ph, "tx").start()
        remote(ph, "mz").wait_recv()
        for c in range(18):
            edge = mix_in[ph, c]
            mixed[ph, 1, c, 0] = jnp.where(low, edge, flip(mixed[ph, 1, c, 1]))
            mixed[ph, 1, c, 1] = jnp.where(low, flip(edge), flip(mixed[ph, 1, c, 2]))
        def seen_z(x):
            m, c = load_matrix(mixed, (ph, 1), x), load_matrix(links[ph], (3,), x)
            if ph == 1:
                traces[8 + x] = real_trace(m, c)
            for p, value in enumerate(twice_traceless(m, c)):
                lower_time[p, x] = value
        loop(2, seen_z)
        for p in range(8):
            time_out[ph, p] = jnp.where(low, lower_time[p, 1], flip(lower_time[p, 0]))
        remote(ph, "tz").start()

        remote(ph, "x2").wait_recv()
        remote(ph, "z0").wait_recv()
        ahead_z(0)
        for x in (1, 0):
            plane(ph, 2, 0, x, load_matrix(lane_ahead, (0,), x), ahead_x(ph, 2, x), 10 + x, split=ph == 1)
            if ph == 0 and x == 1:
                remote(ph, "lx2").start()
        if ph == 0:
            known(0, -2, 2)
        else:
            total = traces[0]
            for slot in range(1, 12):
                total = total + traces[slot]
            gather_z[my_z] = jnp.sum(total, axis=0, keepdims=True)
            pl.semaphore_wait(known_sem.at[1], 2)
            for offset in range(1, half):
                z_sum(offset).start()
            known(2, half)
            for x in (1, 0):
                below(ph, 2, 0, x, load_matrix(links[ph], (2,), x), load_matrix(links[ph], (0,), x),
                      [loops[2, 0, p, x] for p in range(8)])
                if x == 1:
                    remote(ph, "lx2").start()
        pack_lower(0)
        remote(ph, "lz0").start()

        def own(n, x, seen):
            t = conjugated(dagger(load_matrix(links[ph], (n,), x)), seen)
            for p in range(8):
                loops[3, n, p, x] = t[p]
            for p, value in enumerate(conjugated(load_matrix(links[ph], (3,), x), t)):
                lower[ph, 3, n, p, x + 1] = value
        remote(ph, "tx").wait_recv()
        loop(2, lambda x: own(0, x, [lower[ph, 0, 3, p, x + 1] for p in range(8)]))
        if ph == 1:
            for offset in range(1, half):
                z_sum(offset).wait_recv()
            total = gather_z[0]
            for source in range(1, half):
                total = total + gather_z[source]
            gather_rest[my_rest] = total
            pl.semaphore_wait(known_sem.at[2], 1)
            for offset in rest:
                rest_sum(offset).start()
        remote(ph, "tz").wait_recv()
        loop(2, lambda x: own(2, x, [
            jnp.where(low, flip(lower_time[p, x]), pltpu.roll(time_in[ph, p], 64 * x, 1)) for p in range(8)]))

        for name in ("ly", "lx1", "lz1", "lx2", "lz0"):
            remote(ph, name).wait_recv()
        if ph == 0:
            pl.semaphore_wait(known_sem.at[0], 2)
            known(1, -4, 4)

    def half_step(ph, m, x):
        total = [None] * 8
        for n in range(4):
            if n == m:
                continue
            lead = LEAD[min(m, n), max(m, n)]
            first, second = (m, n) if lead == m else (n, m)
            for p in range(8):
                here = loops[first, second, p, x]
                if n == 0:
                    below = lower[ph, 0, m, p, x]
                elif n == 1:
                    edge = jnp.broadcast_to(low_row_in[ph, ROWS.index(m), p, x], (8, 128))
                    below = jnp.where(first_row, edge, pltpu.roll(lower[ph, 1, m, p, x + 1], 1, 0))
                elif n == 2 and m == 3:
                    below = lower_time[p, x]
                elif n == 2:
                    edge = pltpu.roll(low_lane_in[ph, m, p], 64 * x, 1)
                    below = jnp.where(low, edge, flip(lower[ph, 2, m, p, x + 1]))
                else:
                    value = lower[ph, 3, m, p, x + 1]
                    below = jnp.where(first_time, pltpu.roll(value, 65, 1), pltpu.roll(value, 1, 1))
                total[p] = add(total[p], here - below if lead == m else below - here)
        return [moment[m, PARTS[p], x] - (0.5 * KICK) * total[p] for p in range(8)]

    for m in (1, 0):
        loads[m].wait()
        pack_lanes(0, m)
    pl.semaphore_wait(barrier, len(neighbours))
    send_edges(0, 1)
    send_edges(0, 0)
    loads[2].wait()
    send_edges(0, 2)
    loads[3].wait()
    first_half(0)
    loads[4].wait()
    for m in (1, 0, 2, 3):
        def update(x):
            h = half_step(0, m, x)
            for p in range(8):
                moment[m, PARTS[p], x] = h[p]
            u = cayley(h, 0.5 * STEP)
            store_matrix(new_links, (m,), (x,), product(u, load_matrix(old_links, (m,), x)))
        loop(2, update)
        if m in (0, 1):
            pack_lanes(1, m)
        send_edges(1, m)
    first_half(1)

    def finish(x):
        for m in range(4):
            h = half_step(1, m, x)
            for p in range(8):
                final[m, PARTS[p], x] = h[p]
            final[m, 17, x] = -(h[0] + h[1])
            for c, p in ((3, 2), (6, 4), (7, 6)):
                final[m, c, x] = -h[p]
                final[m, 9 + c, x] = h[p + 1]
            for c in (0, 4, 8):
                final[m, c, x] = jnp.zeros((8, 128), F32)
    loop(2, finish)

    for ph in range(2):
        for name in names:
            remote(ph, name).wait_send()
    for offset in range(1, half):
        z_sum(offset).wait_send()
    for offset in rest:
        rest_sum(offset).wait_send()
    for offset in rest:
        rest_sum(offset).wait_recv()
    total = gather_rest[0]
    for source in range(1, len(rest) + 1):
        total = total + gather_rest[source]
    volume = 72.0 * (2 * 8 * 128) * (sizes[0] * sizes[1] * sizes[2])
    plaquette[0, 0] = jnp.sum(total) * (4.0 / volume)


def solution(mesh):
    sizes = tuple(mesh.shape[name] for name in NAMES)
    spec = P(None, None, None, None, "gx", "gy", "zt")

    def step(gauge, momenta):
        shape = gauge.shape
        flat = (4, 18) + shape[4:]
        field = jax.ShapeDtypeStruct(flat, F32)
        dma = pltpu.SemaphoreType.DMA
        vmem = pl.BlockSpec(memory_space=pltpu.VMEM)
        half = sizes[2] // 2
        others = sizes[0] * sizes[1] * 2
        tile = (8, 128)

        def scratch(*lead):
            return pltpu.VMEM(lead + tile, F32)

        def rows(*lead):
            return pltpu.VMEM(lead + (1, 128), F32)

        links, final, plaquette = pl.pallas_call(
            lambda *refs: kernel(sizes, *refs),
            name="md_step",
            out_shape=(field, field, jax.ShapeDtypeStruct((1, 1), F32)),
            in_specs=[pl.BlockSpec(memory_space=pltpu.HBM)] * 2,
            out_specs=(vmem, vmem, pl.BlockSpec(memory_space=pltpu.SMEM)),
            scratch_shapes=[
                scratch(4, 18, 2), scratch(4, 18, 2), scratch(3, 18, 2), scratch(4, 18, 2), scratch(2, 18, 2),
                scratch(2, 2, 18, 3),
                scratch(4, 4, 8, 2), scratch(2, 4, 4, 8, 3), scratch(8, 2),
                rows(2, 3, 18, 2), rows(2, 3, 18, 2), scratch(2, 2, 18), scratch(2, 2, 18), scratch(2, 2, 18),
                scratch(2, 18), scratch(2, 18),
                rows(2, 3, 8, 2), rows(2, 3, 8, 2), scratch(2, 2, 8), scratch(2, 2, 8), scratch(2, 8), scratch(2, 8),
                scratch(12), rows(half), rows(others),
                dma((5,)), dma((2, 14)), dma((2, 14)), dma((half,)), dma((half,)), dma((others,)), dma((others,)),
                pltpu.SemaphoreType.REGULAR((3,)),
            ],
            compiler_params=pltpu.CompilerParams(collective_id=0, has_side_effects=True, vmem_limit_bytes=48 * 1024 * 1024),
        )(*(pltpu.with_memory_space_constraint(a.reshape(flat), pltpu.HBM) for a in (gauge, momenta)))
        return links.reshape(shape), final.reshape(shape), plaquette[0, 0]

    return jax.shard_map(step, mesh=mesh, in_specs=(spec, spec), out_specs=(spec, spec, P()), check_vma=False)
```

time: 55.9 us -> 43.1 us (0.77)
  Pallas kernels: 49.6 us -> 39 us
  local copies, waits for them, and re-layouts: 3.75 us -> 1.63 us
    pallas_call x1, Pallas kernels: 49.6 us -> 39 us  [step(): pl.pallas_call(lambda *refs: kernel(sizes, *refs), name='md_step', out_sh...]
    unnamed x6 -> x2, local copies, waits for them, and re-layouts: 3.75 us -> 1.63 us
where the time goes in v1:
time: 43.1 us; the launch traced here: 42.9 us
  Pallas kernels  39 us (90%)
  between operations  2.33 us (5%)
  local copies, waits for them, and re-layouts  1.63 us (4%)
    pallas_call x1, Pallas kernels, step(): pl.pallas_call(lambda *refs: kernel(sizes, *refs), name='md_step', out_sh...  39 us
    unnamed x2, local copies, waits for them, and re-layouts  1.63 us

profile of v1, /device:TPU:1, one launch (start us, length us, event | category | flops | bytes accessed | tf_op | source)
XLA Modules:
  0.0 42.9 jit_solution(10765510108052089865)
XLA Ops:
  0.6 39.0 %md_step.1 = (f32[4,18,2,8,128]{4,3,2,1,0:T(8,128)S(1)}, f32[4,18,2,8,128]{4,3,2,1,0:T(8,128)S(1)}, f32[1,1]{1,0:T(1,128)}) custom-call(f32[4,18,2,8,128]{4,3,2,1,0:T(8,128)} %bitcast.7, f32[4,18,2,8,128]{4,3,2,1,0:T(8,128)} %bitcast.8), custom_call_target="tpu_custom_call" | custom-call | tf_op jit(solution)/shard_map/md_step/pallas_call | solution.py:566
  39.6 0.8 %copy.8 = f32[4,2,3,3,2,8,128]{6,5,4,3,2,1,0:T(8,128)} copy(f32[4,2,3,3,2,8,128]{6,5,4,3,2,1,0:T(8,128)S(1)} %bitcast.6) | data formatting | bytes 1179648
  40.4 0.8 %copy.9 = f32[4,2,3,3,2,8,128]{6,5,4,3,2,1,0:T(8,128)} copy(f32[4,2,3,3,2,8,128]{6,5,4,3,2,1,0:T(8,128)S(1)} %bitcast.5) | data formatting | bytes 1179648

commit v2 on v1

--- a/solution.py
+++ b/solution.py
@@ -182,14 +182,15 @@
 
 PARTS = (9, 13, 1, 10, 2, 11, 5, 14)
 ROWS = (0, 2, 3)
+LANES = (0, 1, 3)
 
 
 def kernel(
     sizes, gauge, momenta, new_links, final, plaquette,
-    old_links, moment, time_ahead, row_ahead, lane_ahead, mixed,
-    loops, lower, lower_time,
+    old_links, moment, time_ahead, row_ahead, lane_ahead, mixed_x, mixed_z,
+    loops, lower, lower_z,
     row_out, row_in, x_in, lane_out, lane_in, mix_out, mix_in,
-    low_row_out, low_row_in, low_lane_out, low_lane_in, time_out, time_in,
+    low_row_out, low_row_in,
     traces, gather_z, gather_rest,
     load_sem, send_sem, recv_sem, z_send, z_recv, rest_send, rest_recv, known_sem,
 ):
@@ -215,10 +216,10 @@
     for device in neighbours:
         pl.semaphore_signal(barrier, inc=1, device_id=device, device_id_type=MESH)
 
-    loads = {m: pltpu.make_async_copy(gauge.at[m], old_links.at[m], load_sem.at[m]) for m in (1, 0, 2, 3)}
-    loads[4] = pltpu.make_async_copy(momenta, moment, load_sem.at[4])
+    loads = {m: pltpu.make_async_copy(gauge.at[m], old_links.at[m], load_sem.at[m]) for m in (2, 0, 1, 3)}
     for copy in loads.values():
         copy.start()
+    loads[4] = pltpu.make_async_copy(momenta, moment, load_sem.at[4])
 
     def known(step, *offsets):
         for offset in offsets:
@@ -244,21 +245,21 @@
             "y": (2, row_out.at[ph], row_in.at[ph], 1, -1),
             "z0": (3, lane_out.at[ph, 0], lane_in.at[ph, 0], 2, -1),
             "z1": (4, lane_out.at[ph, 1], lane_in.at[ph, 1], 2, -1),
-            "mx": (5, mixed.at[ph, 0, :, 2], mixed.at[ph, 0, :, 0], 0, 1),
-            "mz": (6, mix_out.at[ph], mix_in.at[ph], 2, 1),
-            "lx1": (7, lower.at[ph, 0, 1, :, 2], lower.at[ph, 0, 1, :, 0], 0, 1),
-            "lx2": (8, lower.at[ph, 0, 2, :, 2], lower.at[ph, 0, 2, :, 0], 0, 1),
-            "ly": (9, low_row_out.at[ph], low_row_in.at[ph], 1, 1),
-            "lz0": (10, low_lane_out.at[ph, 0], low_lane_in.at[ph, 0], 2, 1),
-            "lz1": (11, low_lane_out.at[ph, 1], low_lane_in.at[ph, 1], 2, 1),
-            "tx": (12, lower.at[ph, 0, 3, :, 0], lower.at[ph, 0, 3, :, 2], 0, -1),
-            "tz": (13, time_out.at[ph], time_in.at[ph], 2, -1),
+            "z3": (5, lane_out.at[ph, 2], lane_in.at[ph, 2], 2, -1),
+            "mx": (6, mixed_x.at[ph, :, 2], mixed_x.at[ph, :, 0], 0, 1),
+            "mz0": (7, mix_out.at[ph, 0], mix_in.at[ph, 0], 2, 1),
+            "mz1": (8, mix_out.at[ph, 1], mix_in.at[ph, 1], 2, 1),
+            "mz3": (9, mix_out.at[ph, 2], mix_in.at[ph, 2], 2, 1),
+            "lx1": (10, lower.at[ph, 0, 1, :, 2], lower.at[ph, 0, 1, :, 0], 0, 1),
+            "lx2": (11, lower.at[ph, 0, 2, :, 2], lower.at[ph, 0, 2, :, 0], 0, 1),
+            "ly": (12, low_row_out.at[ph], low_row_in.at[ph], 1, 1),
+            "tx": (13, lower.at[ph, 0, 3, :, 0], lower.at[ph, 0, 3, :, 2], 0, -1),
         }[name]
         return pltpu.make_async_remote_copy(
             src_ref=src, dst_ref=dst, send_sem=send_sem.at[ph, number], recv_sem=recv_sem.at[ph, number],
             device_id=peer(axis, offset), device_id_type=MESH)
 
-    names = ("x1", "x2", "y", "z0", "z1", "mx", "mz", "lx1", "lx2", "ly", "lz0", "lz1", "tx", "tz")
+    names = ("x1", "x2", "y", "z0", "z1", "z3", "mx", "mz0", "mz1", "mz3", "lx1", "lx2", "ly", "tx")
 
     def z_sum(offset):
         return pltpu.make_async_remote_copy(
@@ -287,18 +288,20 @@
         d = load_matrix(links[ph], (n,), x)
         right = product(d, c)
         t = twice_traceless(left, right)
-        if ph == 1:
+        if ph == 1 and slot is not None:
             traces[slot] = real_trace(left, right)
         for p in range(8):
             loops[m, n, p, x] = t[p]
         if not split:
-            below(ph, m, n, x, a, d, t)
-
-    def below(ph, m, n, x, a, d, t):
-        for p, value in enumerate(conjugated(d, t)):
-            lower[ph, n, m, p, x + 1] = value
-        for p, value in enumerate(conjugated(a, t)):
-            lower[ph, m, n, p, x + 1] = value
+            below(ph, m, n, x, t)
+
+    def below(ph, m, n, x, t):
+        if n != 2:
+            for p, value in enumerate(conjugated(load_matrix(links[ph], (n,), x), t)):
+                lower[ph, n, m, p, x + 1] = value
+        if m != 2:
+            for p, value in enumerate(conjugated(load_matrix(links[ph], (m,), x), t)):
+                lower[ph, m, n, p, x + 1] = value
 
     def ahead_x(ph, n, x):
         return load_matrix(links[ph], (n,), 1) if x == 0 else load_matrix(x_in, (ph, n - 1))
@@ -308,41 +311,78 @@
             v0 = links[ph][m, c, 0]
             v1 = links[ph][m, c, 1]
             r0 = flip(v0)
-            lane_out[ph, m, c] = jnp.where(low, v1, r0)
+            lane_out[ph, LANES.index(m), c] = jnp.where(low, v1, r0)
             lane_ahead[m, c, 0] = r0
             lane_ahead[m, c, 1] = flip(v1)
 
     def send_edges(ph, m):
-        if m in (0, 1):
+        if m != 2:
             remote(ph, "z" + str(m)).start()
         if m in (1, 2):
             remote(ph, "x" + str(m)).start()
 
     def first_half(ph):
+        field = links[ph]
+
         def shift_time(n, x):
             for c in range(18):
-                v = links[ph][n, c, x]
+                v = field[n, c, x]
                 time_ahead[n, c, x] = jnp.where(last_time, pltpu.roll(v, 63, 1), pltpu.roll(v, 127, 1))
 
-        def mix(d, x):
-            left = product(load_matrix(links[ph], (3,), x), load_matrix(time_ahead, (d,), x))
-            store_matrix(mixed, (ph, d // 2), (x + 1,), dagger_product(load_matrix(links[ph], (d,), x), left))
+        def mix(d, n, x, ahead):
+            left = product(load_matrix(field, (n,), x), ahead)
+            return dagger_product(load_matrix(field, (d,), x), left)
+
+        def mix_z(n, x, ahead):
+            store_matrix(mixed_z, (LANES.index(n),), (x + 1,), mix(2, n, x, ahead))
+
+        def send_mixed(n):
+            k = LANES.index(n)
+            for c in range(18):
+                mix_out[ph, k, c] = jnp.where(low, flip(mixed_z[k, c, 1]), mixed_z[k, c, 2])
+            remote(ph, "mz" + str(n)).start()
+
+        def seen_z(n, slot):
+            k = LANES.index(n)
+            remote(ph, "mz" + str(n)).wait_recv()
+            for c in range(18):
+                edge = mix_in[ph, k, c]
+                mixed_z[k, c, 0] = jnp.where(low, edge, flip(mixed_z[k, c, 1]))
+                mixed_z[k, c, 1] = jnp.where(low, flip(edge), flip(mixed_z[k, c, 2]))
+
+            def seen(x):
+                m, c = load_matrix(mixed_z, (k,), x), load_matrix(field, (n,), x)
+                if ph == 1 and slot is not None:
+                    traces[slot + x] = real_trace(m, c)
+                for p, value in enumerate(twice_traceless(m, c) if n == 3 else twice_traceless(c, m)):
+                    lower_z[k, p, x] = value
+            loop(2, seen)
+
+        def ahead_z(m):
+            for c in range(18):
+                edge = lane_in[ph, LANES.index(m), c]
+                lane_ahead[m, c, 0] = jnp.where(low, lane_ahead[m, c, 0], edge)
+                lane_ahead[m, c, 1] = jnp.where(low, lane_ahead[m, c, 1], flip(edge))
 
         loop(2, lambda x: shift_time(2, x))
-        loop(2, lambda x: mix(2, x))
-        for c in range(18):
-            mix_out[ph, c] = jnp.where(low, flip(mixed[ph, 1, c, 1]), mixed[ph, 1, c, 2])
-        remote(ph, "mz").start()
+        loop(2, lambda x: mix_z(3, x, load_matrix(time_ahead, (2,), x)))
+        send_mixed(3)
 
         def pack_rows(x):
             for k, n in enumerate(ROWS):
                 for c in range(18):
-                    row_out[ph, k, c, x] = links[ph][n, c, x, 0:1, :]
+                    row_out[ph, k, c, x] = field[n, c, x, 0:1, :]
         loop(2, pack_rows)
         remote(ph, "y").start()
+        if ph == 1:
+            pl.semaphore_wait(known_sem.at[0], 2)
+            known(1, -4, 4)
 
         loop(4, lambda i: shift_time(i // 2, lax.rem(i, 2)))
-        loop(2, lambda x: mix(0, x))
+
+        def mix_x(x):
+            store_matrix(mixed_x, (ph,), (x + 1,), mix(0, 3, x, load_matrix(time_ahead, (0,), x)))
+        loop(2, mix_x)
         remote(ph, "mx").start()
 
         remote(ph, "y").wait_recv()
@@ -351,76 +391,49 @@
             k, x = i // 2, lax.rem(i, 2)
             n = k + (k + 1) // 2
             for c in range(18):
-                v = links[ph][n, c, x]
+                v = field[n, c, x]
                 edge = jnp.broadcast_to(row_in[ph, k, c, x], (8, 128))
                 row_ahead[n, c, x] = jnp.where(last_row, edge, pltpu.roll(v, 7, 0))
         loop(6, shift_rows)
+        loop(2, lambda x: mix_z(1, x, load_matrix(row_ahead, (2,), x)))
+        send_mixed(1)
+        remote(ph, "x2").wait_recv()
+        for x in range(2):
+            mix_z(0, x, ahead_x(ph, 2, x))
+        send_mixed(0)
 
         plane(ph, 1, 0, 0, load_matrix(row_ahead, (0,), 0), ahead_x(ph, 1, 0), 0)
         loop(2, lambda x: plane(
             ph, 1, 3, x, load_matrix(row_ahead, (3,), x), load_matrix(time_ahead, (1,), x), 2 + x))
-
         remote(ph, "x1").wait_recv()
         plane(ph, 1, 0, 1, load_matrix(row_ahead, (0,), 1), ahead_x(ph, 1, 1), 1)
         remote(ph, "lx1").start()
 
-        def ahead_z(m):
-            for c in range(18):
-                edge = lane_in[ph, m, c]
-                lane_ahead[m, c, 0] = jnp.where(low, lane_ahead[m, c, 0], edge)
-                lane_ahead[m, c, 1] = jnp.where(low, lane_ahead[m, c, 1], flip(edge))
-
-        def pack_lower(m):
-            for p in range(8):
-                low_lane_out[ph, m, p] = jnp.where(low, flip(lower[ph, 2, m, p, 1]), lower[ph, 2, m, p, 2])
-
-        remote(ph, "z1").wait_recv()
-        ahead_z(1)
-        loop(2, lambda x: plane(
-            ph, 2, 1, x, load_matrix(lane_ahead, (1,), x), load_matrix(row_ahead, (2,), x), 4 + x))
-        pack_lower(1)
-        remote(ph, "lz1").start()
-        for k, m in enumerate(ROWS):
-            for p in range(8):
-                for x in range(2):
-                    low_row_out[ph, k, p, x] = lower[ph, 1, m, p, x + 1, 7:8, :]
-        remote(ph, "ly").start()
-
         remote(ph, "mx").wait_recv()
+
         def seen_x(x):
-            m, c = load_matrix(mixed, (ph, 0), x), load_matrix(links[ph], (3,), x)
+            m, c = load_matrix(mixed_x, (ph,), x), load_matrix(field, (3,), x)
             if ph == 1:
                 traces[6 + x] = real_trace(m, c)
             for p, value in enumerate(twice_traceless(m, c)):
                 lower[ph, 0, 3, p, x] = value
         loop(2, seen_x)
         remote(ph, "tx").start()
-        remote(ph, "mz").wait_recv()
-        for c in range(18):
-            edge = mix_in[ph, c]
-            mixed[ph, 1, c, 0] = jnp.where(low, edge, flip(mixed[ph, 1, c, 1]))
-            mixed[ph, 1, c, 1] = jnp.where(low, flip(edge), flip(mixed[ph, 1, c, 2]))
-        def seen_z(x):
-            m, c = load_matrix(mixed, (ph, 1), x), load_matrix(links[ph], (3,), x)
-            if ph == 1:
-                traces[8 + x] = real_trace(m, c)
-            for p, value in enumerate(twice_traceless(m, c)):
-                lower_time[p, x] = value
-        loop(2, seen_z)
-        for p in range(8):
-            time_out[ph, p] = jnp.where(low, lower_time[p, 1], flip(lower_time[p, 0]))
-        remote(ph, "tz").start()
-
-        remote(ph, "x2").wait_recv()
+
+        seen_z(3, 8)
         remote(ph, "z0").wait_recv()
+        if ph == 0:
+            known(0, -2, 2)
         ahead_z(0)
         for x in (1, 0):
-            plane(ph, 2, 0, x, load_matrix(lane_ahead, (0,), x), ahead_x(ph, 2, x), 10 + x, split=ph == 1)
-            if ph == 0 and x == 1:
+            plane(ph, 2, 0, x, load_matrix(lane_ahead, (0,), x), ahead_x(ph, 2, x), 10 + x)
+            if x == 1:
                 remote(ph, "lx2").start()
-        if ph == 0:
-            known(0, -2, 2)
-        else:
+        remote(ph, "z1").wait_recv()
+        ahead_z(1)
+        loop(2, lambda x: plane(
+            ph, 2, 1, x, load_matrix(lane_ahead, (1,), x), load_matrix(row_ahead, (2,), x), 4 + x, split=ph == 1))
+        if ph == 1:
             total = traces[0]
             for slot in range(1, 12):
                 total = total + traces[slot]
@@ -429,22 +442,21 @@
             for offset in range(1, half):
                 z_sum(offset).start()
             known(2, half)
-            for x in (1, 0):
-                below(ph, 2, 0, x, load_matrix(links[ph], (2,), x), load_matrix(links[ph], (0,), x),
-                      [loops[2, 0, p, x] for p in range(8)])
-                if x == 1:
-                    remote(ph, "lx2").start()
-        pack_lower(0)
-        remote(ph, "lz0").start()
-
-        def own(n, x, seen):
-            t = conjugated(dagger(load_matrix(links[ph], (n,), x)), seen)
+            loop(2, lambda x: below(ph, 2, 1, x, [loops[2, 1, p, x] for p in range(8)]))
+        for k, m in enumerate(ROWS):
             for p in range(8):
-                loops[3, n, p, x] = t[p]
-            for p, value in enumerate(conjugated(load_matrix(links[ph], (3,), x), t)):
-                lower[ph, 3, n, p, x + 1] = value
+                for x in range(2):
+                    low_row_out[ph, k, p, x] = lower[ph, 1, m, p, x + 1, 7:8, :]
+        remote(ph, "ly").start()
+
+        def own_x(x):
+            t = conjugated(dagger(load_matrix(field, (0,), x)), [lower[ph, 0, 3, p, x + 1] for p in range(8)])
+            for p in range(8):
+                loops[3, 0, p, x] = t[p]
+            for p, value in enumerate(conjugated(load_matrix(field, (3,), x), t)):
+                lower[ph, 3, 0, p, x + 1] = value
         remote(ph, "tx").wait_recv()
-        loop(2, lambda x: own(0, x, [lower[ph, 0, 3, p, x + 1] for p in range(8)]))
+        loop(2, own_x)
         if ph == 1:
             for offset in range(1, half):
                 z_sum(offset).wait_recv()
@@ -455,16 +467,15 @@
             pl.semaphore_wait(known_sem.at[2], 1)
             for offset in rest:
                 rest_sum(offset).start()
-        remote(ph, "tz").wait_recv()
-        loop(2, lambda x: own(2, x, [
-            jnp.where(low, flip(lower_time[p, x]), pltpu.roll(time_in[ph, p], 64 * x, 1)) for p in range(8)]))
-
-        for name in ("ly", "lx1", "lz1", "lx2", "lz0"):
+        seen_z(1, None)
+        seen_z(0, None)
+        remote(ph, "z3").wait_recv()
+        ahead_z(3)
+        loop(2, lambda x: plane(
+            ph, 3, 2, x, load_matrix(time_ahead, (2,), x), load_matrix(lane_ahead, (3,), x), None))
+
+        for name in ("lx1", "lx2", "ly"):
             remote(ph, name).wait_recv()
-        if ph == 0:
-            pl.semaphore_wait(known_sem.at[0], 2)
-            known(1, -4, 4)
-
     def half_step(ph, m, x):
         total = [None] * 8
         for n in range(4):
@@ -475,33 +486,32 @@
             for p in range(8):
                 here = loops[first, second, p, x]
                 if n == 0:
-                    below = lower[ph, 0, m, p, x]
+                    below_value = lower[ph, 0, m, p, x]
                 elif n == 1:
                     edge = jnp.broadcast_to(low_row_in[ph, ROWS.index(m), p, x], (8, 128))
-                    below = jnp.where(first_row, edge, pltpu.roll(lower[ph, 1, m, p, x + 1], 1, 0))
-                elif n == 2 and m == 3:
-                    below = lower_time[p, x]
+                    below_value = jnp.where(first_row, edge, pltpu.roll(lower[ph, 1, m, p, x + 1], 1, 0))
                 elif n == 2:
-                    edge = pltpu.roll(low_lane_in[ph, m, p], 64 * x, 1)
-                    below = jnp.where(low, edge, flip(lower[ph, 2, m, p, x + 1]))
+                    below_value = lower_z[LANES.index(m), p, x]
                 else:
                     value = lower[ph, 3, m, p, x + 1]
-                    below = jnp.where(first_time, pltpu.roll(value, 65, 1), pltpu.roll(value, 1, 1))
-                total[p] = add(total[p], here - below if lead == m else below - here)
+                    below_value = jnp.where(first_time, pltpu.roll(value, 65, 1), pltpu.roll(value, 1, 1))
+                total[p] = add(total[p], here - below_value if lead == m else below_value - here)
         return [moment[m, PARTS[p], x] - (0.5 * KICK) * total[p] for p in range(8)]
 
-    for m in (1, 0):
+    loads[2].wait()
+    for m in (0, 1):
         loads[m].wait()
         pack_lanes(0, m)
     pl.semaphore_wait(barrier, len(neighbours))
-    send_edges(0, 1)
-    send_edges(0, 0)
-    loads[2].wait()
-    send_edges(0, 2)
+    for m in (2, 0, 1):
+        send_edges(0, m)
+    loads[4].start()
     loads[3].wait()
+    pack_lanes(0, 3)
+    send_edges(0, 3)
     first_half(0)
     loads[4].wait()
-    for m in (1, 0, 2, 3):
+    for m in (0, 2, 1, 3):
         def update(x):
             h = half_step(0, m, x)
             for p in range(8):
@@ -509,7 +519,7 @@
             u = cayley(h, 0.5 * STEP)
             store_matrix(new_links, (m,), (x,), product(u, load_matrix(old_links, (m,), x)))
         loop(2, update)
-        if m in (0, 1):
+        if m != 2:
             pack_lanes(1, m)
         send_edges(1, m)
     first_half(1)
@@ -540,7 +550,7 @@
     for source in range(1, len(rest) + 1):
         total = total + gather_rest[source]
     volume = 72.0 * (2 * 8 * 128) * (sizes[0] * sizes[1] * sizes[2])
-    plaquette[0, 0] = jnp.sum(total) * (4.0 / volume)
+    plaquette[...] = jnp.broadcast_to(jnp.sum(total) * (4.0 / volume), (8, 128))
 
 
 def solution(mesh):
@@ -566,16 +576,16 @@
         links, final, plaquette = pl.pallas_call(
             lambda *refs: kernel(sizes, *refs),
             name="md_step",
-            out_shape=(field, field, jax.ShapeDtypeStruct((1, 1), F32)),
+            out_shape=(field, field, jax.ShapeDtypeStruct((8, 128), F32)),
             in_specs=[pl.BlockSpec(memory_space=pltpu.HBM)] * 2,
-            out_specs=(vmem, vmem, pl.BlockSpec(memory_space=pltpu.SMEM)),
+            out_specs=(vmem, vmem, vmem),
             scratch_shapes=[
-                scratch(4, 18, 2), scratch(4, 18, 2), scratch(3, 18, 2), scratch(4, 18, 2), scratch(2, 18, 2),
-                scratch(2, 2, 18, 3),
-                scratch(4, 4, 8, 2), scratch(2, 4, 4, 8, 3), scratch(8, 2),
-                rows(2, 3, 18, 2), rows(2, 3, 18, 2), scratch(2, 2, 18), scratch(2, 2, 18), scratch(2, 2, 18),
-                scratch(2, 18), scratch(2, 18),
-                rows(2, 3, 8, 2), rows(2, 3, 8, 2), scratch(2, 2, 8), scratch(2, 2, 8), scratch(2, 8), scratch(2, 8),
+                scratch(4, 18, 2), scratch(4, 18, 2), scratch(3, 18, 2), scratch(4, 18, 2), scratch(4, 18, 2),
+                scratch(2, 18, 3), scratch(3, 18, 3),
+                scratch(4, 4, 8, 2), scratch(2, 4, 4, 8, 3), scratch(3, 8, 2),
+                rows(2, 3, 18, 2), rows(2, 3, 18, 2), scratch(2, 2, 18), scratch(2, 3, 18), scratch(2, 3, 18),
+                scratch(2, 3, 18), scratch(2, 3, 18),
+                rows(2, 3, 8, 2), rows(2, 3, 8, 2),
                 scratch(12), rows(half), rows(others),
                 dma((5,)), dma((2, 14)), dma((2, 14)), dma((half,)), dma((half,)), dma((others,)), dma((others,)),
                 pltpu.SemaphoreType.REGULAR((3,)),

time: 43.1 us -> 41.5 us (0.963)
  between operations: 2.33 us -> 0.64 us
  local copies, waits for them, and re-layouts: 1.63 us -> 2.14 us
    slice x0 -> x1, local copies, waits for them, and re-layouts: none -> 0.51 us  [step(): return (links.reshape(shape), final.reshape(shape), plaquette[0, 0])]
where the time goes in v2:
time: 41.5 us; the launch traced here: 41.4 us
  Pallas kernels  38.6 us (93%)
  local copies, waits for them, and re-layouts  2.14 us (5%)
  between operations  0.64 us (2%)
    pallas_call x1, Pallas kernels, step(): pl.pallas_call(lambda *refs: kernel(sizes, *refs), name='md_step', out_sh...  38.6 us
    unnamed x2, local copies, waits for them, and re-layouts  1.63 us

profile of v2, /device:TPU:1, one launch (start us, length us, event | category | flops | bytes accessed | tf_op | source)
XLA Modules:
  0.0 41.4 jit_solution(14917069342499251442)
XLA Ops:
  0.6 38.6 %md_step.1 = (f32[4,18,2,8,128]{4,3,2,1,0:T(8,128)S(1)}, f32[4,18,2,8,128]{4,3,2,1,0:T(8,128)S(1)}, f32[8,128]{1,0:T(8,128)S(1)}) custom-call(f32[4,18,2,8,128]{4,3,2,1,0:T(8,128)} %bitcast.7, f32[4,18,2,8,128]{4,3,2,1,0:T(8,128)} %bitcast.8), custom_call_target="tpu_custom_call" | custom-call | tf_op jit(solution)/shard_map/md_step/pallas_call | solution.py:576
  39.3 0.5 %slice.3 = f32[1,1]{1,0:T(1,128)} slice(f32[8,128]{1,0:T(8,128)S(1)} %get-tuple-element.8), slice={[0:1], [0:1]} | slice | bytes 8 | tf_op jit(solution)/shard_map/slice | solution.py:595
  39.8 0.8 %copy.7 = f32[4,2,3,3,2,8,128]{6,5,4,3,2,1,0:T(8,128)} copy(f32[4,2,3,3,2,8,128]{6,5,4,3,2,1,0:T(8,128)S(1)} %bitcast.6) | data formatting | bytes 1179648
  40.6 0.8 %copy.8 = f32[4,2,3,3,2,8,128]{6,5,4,3,2,1,0:T(8,128)} copy(f32[4,2,3,3,2,8,128]{6,5,4,3,2,1,0:T(8,128)S(1)} %bitcast.5) | data formatting | bytes 1179648

commit v3 on v2

--- a/solution.py
+++ b/solution.py
@@ -315,11 +315,12 @@
             lane_ahead[m, c, 0] = r0
             lane_ahead[m, c, 1] = flip(v1)
 
-    def send_edges(ph, m):
-        if m != 2:
-            remote(ph, "z" + str(m)).start()
-        if m in (1, 2):
-            remote(ph, "x" + str(m)).start()
+    def send_rows(ph):
+        def pack_rows(x):
+            for k, n in enumerate(ROWS):
+                for c in range(18):
+                    row_out[ph, k, c, x] = links[ph][n, c, x, 0:1, :]
+        loop(2, pack_rows)
 
     def first_half(ph):
         field = links[ph]
@@ -367,13 +368,8 @@
         loop(2, lambda x: shift_time(2, x))
         loop(2, lambda x: mix_z(3, x, load_matrix(time_ahead, (2,), x)))
         send_mixed(3)
-
-        def pack_rows(x):
-            for k, n in enumerate(ROWS):
-                for c in range(18):
-                    row_out[ph, k, c, x] = field[n, c, x, 0:1, :]
-        loop(2, pack_rows)
-        remote(ph, "y").start()
+        pack_lanes(ph, 3)
+        remote(ph, "z3").start()
         if ph == 1:
             pl.semaphore_wait(known_sem.at[0], 2)
             known(1, -4, 4)
@@ -498,20 +494,20 @@
                 total[p] = add(total[p], here - below_value if lead == m else below_value - here)
         return [moment[m, PARTS[p], x] - (0.5 * KICK) * total[p] for p in range(8)]
 
-    loads[2].wait()
-    for m in (0, 1):
+    for m in range(4):
         loads[m].wait()
-        pack_lanes(0, m)
+    send_rows(0)
+    pack_lanes(0, 0)
     pl.semaphore_wait(barrier, len(neighbours))
-    for m in (2, 0, 1):
-        send_edges(0, m)
+    for name in ("y", "x2", "z0"):
+        remote(0, name).start()
+    pack_lanes(0, 1)
+    for name in ("z1", "x1"):
+        remote(0, name).start()
     loads[4].start()
-    loads[3].wait()
-    pack_lanes(0, 3)
-    send_edges(0, 3)
     first_half(0)
     loads[4].wait()
-    for m in (0, 2, 1, 3):
+    for m in (2, 0, 3, 1):
         def update(x):
             h = half_step(0, m, x)
             for p in range(8):
@@ -519,9 +515,17 @@
             u = cayley(h, 0.5 * STEP)
             store_matrix(new_links, (m,), (x,), product(u, load_matrix(old_links, (m,), x)))
         loop(2, update)
-        if m != 2:
-            pack_lanes(1, m)
-        send_edges(1, m)
+        if m == 2:
+            remote(1, "x2").start()
+        elif m == 3:
+            send_rows(1)
+            pack_lanes(1, 0)
+            remote(1, "y").start()
+            remote(1, "z0").start()
+        elif m == 1:
+            pack_lanes(1, 1)
+            remote(1, "z1").start()
+            remote(1, "x1").start()
     first_half(1)
 
     def finish(x):

time: 41.5 us -> 40.9 us (0.986)
  Pallas kernels: 38.6 us -> 38 us
    pallas_call x1, Pallas kernels: 38.6 us -> 38 us  [step(): pl.pallas_call(lambda *refs: kernel(sizes, *refs), name='md_step', out_sh...]
where the time goes in v3:
time: 40.9 us; the launch traced here: 40.8 us
  Pallas kernels  38 us (93%)
  local copies, waits for them, and re-layouts  2.14 us (5%)
  between operations  0.64 us (2%)
    pallas_call x1, Pallas kernels, step(): pl.pallas_call(lambda *refs: kernel(sizes, *refs), name='md_step', out_sh...  38 us
    unnamed x2, local copies, waits for them, and re-layouts  1.63 us

profile of v3, /device:TPU:1, one launch (start us, length us, event | category | flops | bytes accessed | tf_op | source)
XLA Modules:
  0.0 40.8 jit_solution(2958683359786339712)
XLA Ops:
  0.6 38.0 %md_step.1 = (f32[4,18,2,8,128]{4,3,2,1,0:T(8,128)S(1)}, f32[4,18,2,8,128]{4,3,2,1,0:T(8,128)S(1)}, f32[8,128]{1,0:T(8,128)S(1)}) custom-call(f32[4,18,2,8,128]{4,3,2,1,0:T(8,128)} %bitcast.7, f32[4,18,2,8,128]{4,3,2,1,0:T(8,128)} %bitcast.8), custom_call_target="tpu_custom_call" | custom-call | tf_op jit(solution)/shard_map/md_step/pallas_call | solution.py:580
  38.6 0.5 %slice.3 = f32[1,1]{1,0:T(1,128)} slice(f32[8,128]{1,0:T(8,128)S(1)} %get-tuple-element.8), slice={[0:1], [0:1]} | slice | bytes 8 | tf_op jit(solution)/shard_map/slice | solution.py:599
  39.2 0.8 %copy.7 = f32[4,2,3,3,2,8,128]{6,5,4,3,2,1,0:T(8,128)} copy(f32[4,2,3,3,2,8,128]{6,5,4,3,2,1,0:T(8,128)S(1)} %bitcast.6) | data formatting | bytes 1179648
  40.0 0.8 %copy.8 = f32[4,2,3,3,2,8,128]{6,5,4,3,2,1,0:T(8,128)} copy(f32[4,2,3,3,2,8,128]{6,5,4,3,2,1,0:T(8,128)S(1)} %bitcast.5) | data formatting | bytes 1179648

commit v4 on v3

--- a/solution.py
+++ b/solution.py
@@ -186,7 +186,7 @@
 
 
 def kernel(
-    sizes, gauge, momenta, new_links, final, plaquette,
+    sizes, gauge, momenta, fields, plaquette,
     old_links, moment, time_ahead, row_ahead, lane_ahead, mixed_x, mixed_z,
     loops, lower, lower_z,
     row_out, row_in, x_in, lane_out, lane_in, mix_out, mix_in,
@@ -195,6 +195,7 @@
     load_sem, send_sem, recv_sem, z_send, z_recv, rest_send, rest_recv, known_sem,
 ):
     me = [lax.axis_index(name) for name in NAMES]
+    new_links, final = fields.at[0], fields.at[1]
     links = (old_links, new_links)
     half = sizes[2] // 2
     my_half, my_z = me[2] // half, lax.rem(me[2], half)
@@ -564,7 +565,6 @@
     def step(gauge, momenta):
         shape = gauge.shape
         flat = (4, 18) + shape[4:]
-        field = jax.ShapeDtypeStruct(flat, F32)
         dma = pltpu.SemaphoreType.DMA
         vmem = pl.BlockSpec(memory_space=pltpu.VMEM)
         half = sizes[2] // 2
@@ -577,12 +577,12 @@
         def rows(*lead):
             return pltpu.VMEM(lead + (1, 128), F32)
 
-        links, final, plaquette = pl.pallas_call(
+        fields, plaquette = pl.pallas_call(
             lambda *refs: kernel(sizes, *refs),
             name="md_step",
-            out_shape=(field, field, jax.ShapeDtypeStruct((8, 128), F32)),
+            out_shape=(jax.ShapeDtypeStruct((2,) + flat, F32), jax.ShapeDtypeStruct((8, 128), F32)),
             in_specs=[pl.BlockSpec(memory_space=pltpu.HBM)] * 2,
-            out_specs=(vmem, vmem, vmem),
+            out_specs=(vmem, vmem),
             scratch_shapes=[
                 scratch(4, 18, 2), scratch(4, 18, 2), scratch(3, 18, 2), scratch(4, 18, 2), scratch(4, 18, 2),
                 scratch(2, 18, 3), scratch(3, 18, 3),
@@ -596,6 +596,6 @@
             ],
             compiler_params=pltpu.CompilerParams(collective_id=0, has_side_effects=True, vmem_limit_bytes=48 * 1024 * 1024),
         )(*(pltpu.with_memory_space_constraint(a.reshape(flat), pltpu.HBM) for a in (gauge, momenta)))
-        return links.reshape(shape), final.reshape(shape), plaquette[0, 0]
+        return fields[0].reshape(shape), fields[1].reshape(shape), plaquette[0, 0]
 
     return jax.shard_map(step, mesh=mesh, in_specs=(spec, spec), out_specs=(spec, spec, P()), check_vma=False)

time: 40.9 us -> 40.3 us (0.985)
  local copies, waits for them, and re-layouts: 2.14 us -> 1.6 us
    unnamed x2 -> x0, local copies, waits for them, and re-layouts: 1.63 us -> none
    slice x1 -> x2, local copies, waits for them, and re-layouts: 0.51 us -> 1.6 us  [step(): return (fields[0].reshape(shape), fields[1].reshape(shape), plaquette[0, 0])]
where the time goes in v4:
time: 40.3 us; the launch traced here: 40.2 us
  Pallas kernels  38 us (94%)
  local copies, waits for them, and re-layouts  1.6 us (4%)
  between operations  0.64 us (2%)
    pallas_call x1, Pallas kernels, step(): pl.pallas_call(lambda *refs: kernel(sizes, *refs), name='md_step', out_sh...  38 us
    slice x2, local copies, waits for them, and re-layouts, step(): return (fields[0].reshape(shape), fields[1].reshape(shape), plaquette[0, 0])  1.6 us

profile of v4, /device:TPU:1, one launch (start us, length us, event | category | flops | bytes accessed | tf_op | source)
XLA Modules:
  0.0 40.2 jit_solution(7665226588195347326)
XLA Ops:
  0.6 38.0 %md_step.1 = (f32[2,4,18,2,8,128]{5,4,3,2,1,0:T(8,128)S(1)}, f32[8,128]{1,0:T(8,128)S(1)}) custom-call(f32[4,18,2,8,128]{4,3,2,1,0:T(8,128)} %bitcast.5, f32[4,18,2,8,128]{4,3,2,1,0:T(8,128)} %bitcast.6), custom_call_target="tpu_custom_call" | custom-call | tf_op jit(solution)/shard_map/md_step/pallas_call | solution.py:580
  38.6 0.5 %slice.11 = f32[1,1]{1,0:T(1,128)} slice(f32[8,128]{1,0:T(8,128)S(1)} %get-tuple-element.6), slice={[0:1], [0:1]} | slice | bytes 8 | tf_op jit(solution)/shard_map/slice | solution.py:599
  39.2 1.1 %fusion = (f32[1,4,18,2,8,128]{5,4,3,2,1,0:T(8,128)}, f32[1,4,18,2,8,128]{5,4,3,2,1,0:T(8,128)}) fusion(f32[2,4,18,2,8,128]{5,4,3,2,1,0:T(8,128)S(1)} %get-tuple-element.5), kind=kLoop, calls=%fused_computation | loop fusion | bytes 2359296 | tf_op jit(solution)/shard_map/slice | solution.py:599
